TPU v7x, 512 devices: a whole 4x4x16 slice. The times are simulated.
512 devices in a mesh: dp: 128 (over y, x, z_hi, core), mp: 4 (over z_lo).
Axes of the slice: x: 4, y: 4, z: 16 (z_hi: 4, z_lo: 4; z = z_hi * 4 + z_lo), core: 2. Of those that a mesh axis runs over, the one named last changes fastest.
Arguments:
- layer_input: bfloat16 [512, 8192], P('dp'), may hold values from -6 to 6
- pre_act: bfloat16 [512, 8192], P('dp', 'mp'), may hold values from -8 to 8
- hidden_adjoint: bfloat16 [512, 8192], P('dp', 'mp'), may hold values from -6 to 6
- output_adjoint: bfloat16 [512, 8192], P('dp', 'mp'), may hold values from -6 to 6
Outputs:
- precond_in: float32 [8192, 8192], P('dp', 'mp')
- direction_in: float32 [8192, 8192], P('dp', 'mp')
- precond_out: float32 [8192, 8192], P('dp', 'mp')
- direction_out: float32 [8192, 8192], P('dp', 'mp')
- sq_norm: float32 [], replicated
All inputs are finite; a program needn't handle non-finite values.
Results may differ from a plain program's by a relative error of at most 0.0029.
Values may be sent and summed in bfloat16 or wider, within the bound.
A program may use at most 64 MiB of HBM per device.

v0:
```python
import jax
import jax.numpy as jnp
from jax import lax
from jax.sharding import Mesh
from jax.sharding import PartitionSpec as P

D = 8192
H = 8192
DP = ("dp_0", "dp_1", "dp_2", "dp_3")
DP_MP = ("dp_0", "dp_1", "dp_2", "dp_3", "mp")
DAMPING = 0.1
EXPONENT = 0.75


def in_order(pieces, dim):
    pieces = jnp.moveaxis(pieces, 0, dim)
    lengths = pieces.shape
    return pieces.reshape(*lengths[:dim], lengths[dim] * lengths[dim + 1], *lengths[dim + 2 :])


def copy_for_each(x, axis):
    size = lax.axis_size(axis)
    return lax.all_to_all(jnp.broadcast_to(x[None], (size, *x.shape)), axis, 0, 0, tiled=True)


def gather_directly(x, axis, dim):
    return in_order(copy_for_each(x, axis), dim)


def split_up(x, dim, size):
    before, after = (x.shape[:dim], x.shape[dim + 1 :])
    return jnp.moveaxis(x.reshape(*before, size, -1, *after), dim, 0)


def exchange_in_order(pieces, axes, turns):
    lengths = [lax.axis_size(a) for a in axes]
    pieces = pieces.reshape(*lengths, *pieces.shape[1:])
    for k in turns:
        pieces = lax.all_to_all(pieces, axes[k], split_axis=k, concat_axis=k, tiled=True)
    return pieces.reshape(-1, *pieces.shape[len(axes) :])


def two_step_exchange(x, groups, turns, split_dim, concat_dim):
    size = lax.axis_size(groups[0]) * lax.axis_size(groups[1])
    pieces = split_up(x, split_dim, size)
    return in_order(exchange_in_order(pieces, groups, turns), concat_dim)


def side_by_side(arrays, axis, dim, along):
    ends, at = ([], 0)
    for a in arrays[:-1]:
        at += a.shape[along]
        ends.append(at)
    both = jnp.concatenate(arrays, axis=along)
    return tuple(jnp.split(lax.all_gather(both, axis, axis=dim, tiled=True), ends, axis=along))


def over_axes(x, axes):
    for axis in axes:
        x = lax.psum(x, axis)
    return x


def square_bf(values):
    wide = values.astype(jnp.float32)
    return (wide * wide).astype(jnp.bfloat16)


def accumulate(act_block, sq_block, adj_piece):
    contract = (((0,), (0,)), ((), ()))
    grad_sum = lax.dot_general(act_block, adj_piece, contract, preferred_element_type=jnp.float32)
    square_sum = lax.dot_general(
        sq_block, square_bf(adj_piece), contract, preferred_element_type=jnp.float32
    )
    return (grad_sum, square_sum)


def finish(partial_value, total_rows):
    gradient = partial_value[0] / total_rows
    precond = (partial_value[1] / total_rows + DAMPING) ** EXPONENT
    norm_term = jnp.sum(gradient * gradient / precond)
    return (gradient, precond, norm_term)


def shards(layer_input, pre_act, hidden_adjoint, output_adjoint):
    preact = pre_act.astype(jnp.float32)
    logistic = jax.nn.sigmoid(preact)
    hidden = (preact * logistic).astype(jnp.bfloat16)
    adjoint = (
        hidden_adjoint.astype(jnp.float32) * logistic * (1.0 + preact * (1.0 - logistic))
    ).astype(jnp.bfloat16)
    own_input = lax.all_to_all(layer_input, DP, split_axis=1, concat_axis=0, tiled=True)
    sq_input = square_bf(own_input)
    total_rows = own_input.shape[0]
    wide_hidden = gather_directly(hidden, "mp", 1)
    own_hidden = two_step_exchange(wide_hidden, (("dp_0", "dp_1", "dp_2"), "dp_3"), (1, 0), 1, 0)
    sq_hidden = square_bf(own_hidden)
    pieces = side_by_side((adjoint, output_adjoint), DP, 0, 1)
    first_part = accumulate(own_input, sq_input, pieces[0])
    second_part = accumulate(own_hidden, sq_hidden, pieces[1])
    gradient_in, precond_in, term_in = finish(first_part, total_rows)
    gradient_out, precond_out, term_out = finish(second_part, total_rows)
    sq_norm = over_axes(term_in + term_out, DP_MP)
    rescale = jnp.sqrt(2.0 * D * H / sq_norm)
    direction_in = gradient_in / precond_in * rescale
    direction_out = gradient_out / precond_out * rescale
    return (precond_in, direction_in, precond_out, direction_out, sq_norm)


def solution(mesh):
    torus = Mesh(
        mesh.devices.reshape(4, 4, 4, 2, mesh.shape["mp"]), ("dp_0", "dp_1", "dp_2", "dp_3", "mp")
    )
    placed = (P(DP, None), P(DP, "mp"), P(DP, "mp"), P(DP, "mp"))
    return jax.shard_map(
        shards,
        mesh=torus,
        in_specs=placed,
        out_specs=(P(DP, "mp"), P(DP, "mp"), P(DP, "mp"), P(DP, "mp"), P()),
        check_vma=False,
    )
```

profile of v0, /device:TPU:32, one launch (start us, length us, event | category | flops | bytes accessed | tf_op | source)
XLA Modules:
  0.0 210.1 jit_solution(18236963314669672673)
XLA Ops:
  7.2 0.8 fusion.13
  8.0 1.3 maximum_bitcast_fusion
  9.4 0.6 broadcast_in_dim.2
  10.0 8.7 %all-to-all-start.1 = ((bf16[4,4,2048]{2,1,0:T(4,128)(2,1)}), bf16[4,4,2048]{2,1,0:T(4,128)(2,1)S(1)}, u32[]{:S(2)}, u32[]{:S(2)}) async-start(bf16[4,4,2048]{2,1,0:T(4,128)(2,1)} %broadcast_in_dim.2), calls=%async_computation.1 | async-start | bytes 131072 | tf_op jit(solution)/shard_map/all_to_all | solution.py:23
  18.7 1.0 all_to_all.23
  19.8 0.7 reshape.20
  20.6 2.8 %all-to-all-done.1 = bf16[4,4,2048]{2,1,0:T(4,128)(2,1)S(1)} async-done(((bf16[4,4,2048]{2,1,0:T(4,128)(2,1)}), bf16[4,4,2048]{2,1,0:T(4,128)(2,1)S(1)}, u32[]{:S(2)}, u32[]{:S(2)}) %all-to-all-start.1) | async-done | bytes 65568 | tf_op jit(solution)/shard_map/all_to_all | solution.py:23
  23.9 3.8 %all_to_all.34 = bf16[2,2,8192]{2,1,0:T(2,128)(2,1)S(1)} all-to-all(bf16[2,2,8192]{2,1,0:T(2,128)(2,1)S(1)} %reshape.22), channel_id=1, replica_groups=mesh['dp_0'=4,'dp_1'=4,'dp_2'=4,'dp_3'=2,'mp'=4] {'dp_3'}, dimensions={0} | all-to-all | bytes 131072 | tf_op jit(solution)/shard_map/all_to_all | solution.py:39
  27.7 17.1 %all-to-all-start = ((bf16[128,2,128]{2,1,0:T(2,128)(2,1)}), bf16[128,2,128]{2,1,0:T(2,128)(2,1)S(1)}, u32[]{:S(2)}, u32[]{:S(2)}) async-start(bf16[128,2,128]{2,1,0:T(2,128)(2,1)} %reshape.20), calls=%async_computation | async-start | bytes 131072 | tf_op jit(solution)/shard_map/all_to_all | solution.py:92
  44.9 0.8 reshape.24
  45.7 16.7 %all-to-all-done = bf16[128,2,128]{2,1,0:T(2,128)(2,1)S(1)} async-done(((bf16[128,2,128]{2,1,0:T(2,128)(2,1)}), bf16[128,2,128]{2,1,0:T(2,128)(2,1)S(1)}, u32[]{:S(2)}, u32[]{:S(2)}) %all-to-all-start) | async-done | bytes 65568 | tf_op jit(solution)/shard_map/all_to_all | solution.py:92
  62.4 4.6 %all-to-all-start.3 = ((bf16[64,2,256]{2,1,0:T(2,128)(2,1)}), bf16[64,2,256]{2,1,0:T(2,128)(2,1)S(1)}, u32[]{:S(2)}, u32[]{:S(2)}) async-start(bf16[64,2,256]{2,1,0:T(2,128)(2,1)} %reshape.24), calls=%async_computation.3 | async-start | bytes 131072 | tf_op jit(solution)/shard_map/all_to_all | solution.py:39
  67.1 18.8 %all-to-all-done.3 = bf16[64,2,256]{2,1,0:T(2,128)(2,1)S(1)} async-done(((bf16[64,2,256]{2,1,0:T(2,128)(2,1)}), bf16[64,2,256]{2,1,0:T(2,128)(2,1)S(1)}, u32[]{:S(2)}, u32[]{:S(2)}) %all-to-all-start.3) | async-done | bytes 65568 | tf_op jit(solution)/shard_map/all_to_all | solution.py:39
  86.1 47.5 %all-gather.3.cloned.1.call-done = bf16[128,4,4096]{2,1,0:T(4,128)(2,1)} async-done(((bf16[1,4,4096]{2,1,0:T(4,128)(2,1)}), bf16[128,4,4096]{2,1,0:T(4,128)(2,1)}) %all-gather.3.cloned.1.call-update) | async-done | bytes 4194320 | tf_op jit(solution)/shard_map/all_gather | solution.py:55
  133.6 6.9 %reshape.19 = bf16[512,4096]{1,0:T(8,128)(2,1)} reshape(bf16[128,4,4096]{2,1,0:T(4,128)(2,1)} %all-gather.3.cloned.1.call-done) | data formatting | bytes 8388608
  140.5 2.3 %fusion = f32[64,2048]{1,0:T(8,128)S(1)} fusion(bf16[512,4096]{1,0:T(8,128)(2,1)} %reshape.19, bf16[512,64]{1,0:T(8,128)(2,1)S(1)} %bitcast.29), kind=kOutput, calls=%fused_computation.6 | convolution fusion | flops 137723904 | bytes 2686976 | tf_op jit(solution)/shard_map/dot_general | solution.py:72
  142.8 2.9 %multiply_reduce_fusion.1 = (f32[]{:T(128)}, f32[64,2048]{1,0:T(8,128)S(1)}) fusion(f32[64,2048]{1,0:T(8,128)S(1)} %fusion, bf16[512,64]{1,0:T(8,128)(2,1)S(1)} %bitcast.30, bf16[512,4096]{1,0:T(8,128)(2,1)} %reshape.19), kind=kOutput, calls=%fused_computation.15 | convolution fusion | flops 134742016 | bytes 3211268 | tf_op jit(solution)/shard_map/dot_general | solution.py:71
  146.3 1.2 multiply_reduce_fusion
  148.8 11.3 %psum.35 = f32[]{:T(128)} all-reduce(f32[]{:T(128)S(6)} %add.29), channel_id=1, replica_groups=mesh['dp_0'=4,'dp_1'=4,'dp_2'=4,'dp_3'=2,'mp'=4] {'dp_0'}, use_global_device_ids=true, to_apply=%region_2.0 | all-reduce | flops 1 | bytes 8 | tf_op jit(solution)/shard_map/psum | solution.py:60
  160.1 11.0 %psum.36 = f32[]{:T(128)} all-reduce(f32[]{:T(128)} %psum.35), channel_id=1, replica_groups=mesh['dp_0'=4,'dp_1'=4,'dp_2'=4,'dp_3'=2,'mp'=4] {'dp_1'}, use_global_device_ids=true, to_apply=%region_3.0 | all-reduce | flops 1 | bytes 8 | tf_op jit(solution)/shard_map/psum | solution.py:60
  171.2 14.1 %psum.37 = f32[]{:T(128)} all-reduce(f32[]{:T(128)} %psum.36), channel_id=1, replica_groups=mesh['dp_0'=4,'dp_1'=4,'dp_2'=4,'dp_3'=2,'mp'=4] {'dp_2'}, use_global_device_ids=true, to_apply=%region_4.0 | all-reduce | flops 1 | bytes 8 | tf_op jit(solution)/shard_map/psum | solution.py:60
  185.3 3.1 %psum.38 = f32[]{:T(128)} all-reduce(f32[]{:T(128)} %psum.37), channel_id=1, replica_groups=mesh['dp_0'=4,'dp_1'=4,'dp_2'=4,'dp_3'=2,'mp'=4] {'dp_3'}, use_global_device_ids=true, to_apply=%region_5.0 | all-reduce | flops 1 | bytes 8 | tf_op jit(solution)/shard_map/psum | solution.py:60
  188.3 12.2 %psum.39 = f32[]{:T(128)} all-reduce(f32[]{:T(128)} %psum.38), channel_id=1, replica_groups=mesh['dp_0'=4,'dp_1'=4,'dp_2'=4,'dp_3'=2,'mp'=4] {'mp'}, use_global_device_ids=true, to_apply=%region_6.0 | all-reduce | flops 1 | bytes 8 | tf_op jit(solution)/shard_map/psum | solution.py:60
  201.3 2.0 multiply_multiply_fusion
  (14 shorter events, 1.7 us)
Async XLA Ops:
  7.2 126.4 %all-gather.3.cloned.1.call-start = ((), (), s32[]{:S(2)}) async-start(), calls=%async_computation.4 | async-start | bytes 4227072 | tf_op jit(solution)/shard_map/all_gather | solution.py:55
  10.0 13.3 %all-to-all-start.1 = ((bf16[4,4,2048]{2,1,0:T(4,128)(2,1)}), bf16[4,4,2048]{2,1,0:T(4,128)(2,1)S(1)}, u32[]{:S(2)}, u32[]{:S(2)}) async-start(bf16[4,4,2048]{2,1,0:T(4,128)(2,1)} %broadcast_in_dim.2), calls=%async_computation.1 | async-start | bytes 131072 | tf_op jit(solution)/shard_map/all_to_all | solution.py:23
  27.7 34.7 %all-to-all-start = ((bf16[128,2,128]{2,1,0:T(2,128)(2,1)}), bf16[128,2,128]{2,1,0:T(2,128)(2,1)S(1)}, u32[]{:S(2)}, u32[]{:S(2)}) async-start(bf16[128,2,128]{2,1,0:T(2,128)(2,1)} %reshape.20), calls=%async_computation | async-start | bytes 131072 | tf_op jit(solution)/shard_map/all_to_all | solution.py:92
  62.4 23.5 %all-to-all-start.3 = ((bf16[64,2,256]{2,1,0:T(2,128)(2,1)}), bf16[64,2,256]{2,1,0:T(2,128)(2,1)S(1)}, u32[]{:S(2)}, u32[]{:S(2)}) async-start(bf16[64,2,256]{2,1,0:T(2,128)(2,1)} %reshape.24), calls=%async_computation.3 | async-start | bytes 131072 | tf_op jit(solution)/shard_map/all_to_all | solution.py:39
  140.5 5.2 %copy-start = (bf16[512,4096]{1,0:T(8,128)(2,1)S(1)}, bf16[512,4096]{1,0:T(8,128)(2,1)}, u32[]{:S(2)}) copy-start(bf16[512,4096]{1,0:T(8,128)(2,1)} %reshape.19) | copy-start | bytes 12582916
Sparse Core Ops, SparseCore 0:
  13.0 120.5 all-gather.2
where the time goes:
time: 211 us; the launch traced here: 210 us
  waiting for transfers between devices  85.8 us (41%)
  blocking collectives  55.5 us (26%)
  starting transfers between devices  30.4 us (14%)
  between operations  16.1 us (8%)
  local copies, waits for them, and re-layouts  11.1 us (5%)
  matrix products  7.01 us (3%)
  other arithmetic  4.16 us (2%)
    psum x5, blocking collectives, over_axes(): x = lax.psum(x, axis)  51.7 us
    all_gather x1, waiting for transfers between devices, side_by_side(): lax.all_gather(both, axis, axis=dim, tiled=True)  47.5 us
    all_to_all x1, waiting for transfers between devices, exchange_in_order(): lax.all_to_all(pieces, axes[k], split_axis=k, concat_axis=k, tiled=True)  18.8 us
    all_to_all x1, starting transfers between devices, shards(): lax.all_to_all(layer_input, DP, split_axis=1, concat_axis=0, tiled=True)  17.1 us
    all_to_all x1, waiting for transfers between devices, shards(): lax.all_to_all(layer_input, DP, split_axis=1, concat_axis=0, tiled=True)  16.7 us
    unnamed x9, local copies, waits for them, and re-layouts  8.99 us
    all_to_all x1, starting transfers between devices, copy_for_each(): lax.all_to_all(jnp.broadcast_to(x[None], (size, *x.shape)), axis, 0, 0, t...  8.71 us
    all_to_all x1, starting transfers between devices, exchange_in_order(): lax.all_to_all(pieces, axes[k], split_axis=k, concat_axis=k, tiled=True)  4.62 us
  transfers between devices with their start and end apart: 4, of which 4 were waited for; matrix products, arithmetic and copies ran while one was open for 2% of the time, Pallas kernels for 0%

commit v1 on v0

--- a/solution.py
+++ b/solution.py
@@ -10,6 +10,7 @@
 DP_MP = ("dp_0", "dp_1", "dp_2", "dp_3", "mp")
 DAMPING = 0.1
 EXPONENT = 0.75
+_raise_heads = lambda xs, device_axis: jnp.sum(lax.all_gather(xs, device_axis), 0)
 
 
 def in_order(pieces, dim):
@@ -57,7 +58,7 @@
 
 def over_axes(x, axes):
     for axis in axes:
-        x = lax.psum(x, axis)
+        x = _raise_heads(x, axis)
     return x
 
 

time: 211 us -> 222 us (1.052)
  local copies, waits for them, and re-layouts: 11.1 us -> 23.8 us
  blocking collectives: 55.5 us -> 52.4 us
  other arithmetic: 4.16 us -> 7.18 us
    psum x5 -> x0, blocking collectives: 51.7 us -> none  [over_axes(): x = lax.psum(x, axis)]
    unnamed x0 -> x5, blocking collectives: none -> 48.6 us
    unnamed x9 -> x24, local copies, waits for them, and re-layouts: 8.99 us -> 21.7 us
    reduce_sum x0 -> x5, other arithmetic: none -> 3.02 us  [jnp.sum(lax.all_gather(xs, device_axis), 0)]
where the time goes in v1:
time: 222 us; the launch traced here: 221 us
  waiting for transfers between devices  84.5 us (38%)
  blocking collectives  52.4 us (24%)
  starting transfers between devices  30.4 us (14%)
  local copies, waits for them, and re-layouts  23.8 us (11%)
  between operations  16.2 us (7%)
  other arithmetic  7.18 us (3%)
  matrix products  7.02 us (3%)
    unnamed x5, blocking collectives  48.6 us
    all_gather x1, waiting for transfers between devices, side_by_side(): lax.all_gather(both, axis, axis=dim, tiled=True)  47.5 us
    unnamed x24, local copies, waits for them, and re-layouts  21.7 us
    all_to_all x1, waiting for transfers between devices, exchange_in_order(): lax.all_to_all(pieces, axes[k], split_axis=k, concat_axis=k, tiled=True)  17.5 us
    all_to_all x1, starting transfers between devices, shards(): lax.all_to_all(layer_input, DP, split_axis=1, concat_axis=0, tiled=True)  17.1 us
    all_to_all x1, waiting for transfers between devices, shards(): lax.all_to_all(layer_input, DP, split_axis=1, concat_axis=0, tiled=True)  16.7 us
    all_to_all x1, starting transfers between devices, copy_for_each(): lax.all_to_all(jnp.broadcast_to(x[None], (size, *x.shape)), axis, 0, 0, t...  8.71 us
    all_to_all x1, starting transfers between devices, exchange_in_order(): lax.all_to_all(pieces, axes[k], split_axis=k, concat_axis=k, tiled=True)  4.62 us
  transfers between devices with their start and end apart: 4, of which 4 were waited for; matrix products, arithmetic and copies ran while one was open for 2% of the time, Pallas kernels for 0%

profile of v1, /device:TPU:32, one launch (start us, length us, event | category | flops | bytes accessed | tf_op | source)
XLA Modules:
  0.0 221.5 jit_solution(8277706337043241596)
XLA Ops:
  8.0 1.3 maximum_bitcast_fusion
  10.0 8.7 %all-to-all-start.1 = ((bf16[4,4,2048]{2,1,0:T(4,128)(2,1)}), bf16[4,4,2048]{2,1,0:T(4,128)(2,1)S(1)}, u32[]{:S(2)}, u32[]{:S(2)}) async-start(bf16[4,4,2048]{2,1,0:T(4,128)(2,1)} %broadcast_in_dim.2), calls=%async_computation.1 | async-start | bytes 131072 | tf_op jit(solution)/shard_map/all_to_all | solution.py:24
  20.6 2.8 %all-to-all-done.1 = bf16[4,4,2048]{2,1,0:T(4,128)(2,1)S(1)} async-done(((bf16[4,4,2048]{2,1,0:T(4,128)(2,1)}), bf16[4,4,2048]{2,1,0:T(4,128)(2,1)S(1)}, u32[]{:S(2)}, u32[]{:S(2)}) %all-to-all-start.1) | async-done | bytes 65568 | tf_op jit(solution)/shard_map/all_to_all | solution.py:24
  23.9 3.8 %all_to_all.34 = bf16[2,2,8192]{2,1,0:T(2,128)(2,1)S(1)} all-to-all(bf16[2,2,8192]{2,1,0:T(2,128)(2,1)S(1)} %reshape.47), channel_id=1, replica_groups=mesh['dp_0'=4,'dp_1'=4,'dp_2'=4,'dp_3'=2,'mp'=4] {'dp_3'}, dimensions={0} | all-to-all | bytes 131072 | tf_op jit(solution)/shard_map/all_to_all | solution.py:40
  27.7 17.1 %all-to-all-start = ((bf16[128,2,128]{2,1,0:T(2,128)(2,1)}), bf16[128,2,128]{2,1,0:T(2,128)(2,1)S(1)}, u32[]{:S(2)}, u32[]{:S(2)}) async-start(bf16[128,2,128]{2,1,0:T(2,128)(2,1)} %reshape.45), calls=%async_computation | async-start | bytes 131072 | tf_op jit(solution)/shard_map/all_to_all | solution.py:93
  45.7 16.7 %all-to-all-done = bf16[128,2,128]{2,1,0:T(2,128)(2,1)S(1)} async-done(((bf16[128,2,128]{2,1,0:T(2,128)(2,1)}), bf16[128,2,128]{2,1,0:T(2,128)(2,1)S(1)}, u32[]{:S(2)}, u32[]{:S(2)}) %all-to-all-start) | async-done | bytes 65568 | tf_op jit(solution)/shard_map/all_to_all | solution.py:93
  62.4 4.6 %all-to-all-start.3 = ((bf16[64,2,256]{2,1,0:T(2,128)(2,1)}), bf16[64,2,256]{2,1,0:T(2,128)(2,1)S(1)}, u32[]{:S(2)}, u32[]{:S(2)}) async-start(bf16[64,2,256]{2,1,0:T(2,128)(2,1)} %reshape.49), calls=%async_computation.3 | async-start | bytes 131072 | tf_op jit(solution)/shard_map/all_to_all | solution.py:40
  67.0 1.3 dynamic-slice
  68.4 17.5 %all-to-all-done.3 = bf16[64,2,256]{2,1,0:T(2,128)(2,1)S(1)} async-done(((bf16[64,2,256]{2,1,0:T(2,128)(2,1)}), bf16[64,2,256]{2,1,0:T(2,128)(2,1)S(1)}, u32[]{:S(2)}, u32[]{:S(2)}) %all-to-all-start.3) | async-done | bytes 65568 | tf_op jit(solution)/shard_map/all_to_all | solution.py:40
  86.1 47.5 %all-gather.3.cloned.1.call-done = bf16[128,4,4096]{2,1,0:T(4,128)(2,1)} async-done(((bf16[1,4,4096]{2,1,0:T(4,128)(2,1)}), bf16[128,4,4096]{2,1,0:T(4,128)(2,1)}) %all-gather.3.cloned.1.call-update) | async-done | bytes 4194320 | tf_op jit(solution)/shard_map/all_gather | solution.py:56
  133.6 6.9 %reshape.34 = bf16[512,4096]{1,0:T(8,128)(2,1)} reshape(bf16[128,4,4096]{2,1,0:T(4,128)(2,1)} %all-gather.3.cloned.1.call-done) | data formatting | bytes 8388608
  140.5 2.3 %fusion.2 = f32[64,2048]{1,0:T(8,128)S(1)} fusion(bf16[512,4096]{1,0:T(8,128)(2,1)} %reshape.34, bf16[512,64]{1,0:T(8,128)(2,1)S(1)} %bitcast.32), kind=kOutput, calls=%fused_computation.8 | convolution fusion | flops 137723904 | bytes 2686976 | tf_op jit(solution)/shard_map/dot_general | solution.py:73
  142.8 2.8 %multiply_reduce_fusion = (f32[]{:T(128)}, f32[64,2048]{1,0:T(8,128)S(1)}) fusion(f32[64,2048]{1,0:T(8,128)S(1)} %fusion.2, bf16[512,64]{1,0:T(8,128)(2,1)S(1)} %bitcast.33, bf16[512,4096]{1,0:T(8,128)(2,1)} %reshape.34), kind=kOutput, calls=%fused_computation.14 | convolution fusion | flops 134742016 | bytes 3211268 | tf_op jit(solution)/shard_map/dot_general | solution.py:72
  146.2 1.3 multiply_reduce_fusion.1
  150.8 10.8 %all-reduce = f32[4]{0:T(128)S(1)} all-reduce(f32[4]{0:T(128)S(1)} %dynamic-update-slice), channel_id=1, replica_groups=mesh['dp_0'=4,'dp_1'=4,'dp_2'=4,'dp_3'=2,'mp'=4] {'dp_0'}, use_global_device_ids=true, to_apply=%add | all-reduce | flops 4 | bytes 32
  162.2 1.4 dynamic-update-slice.1
  164.9 10.4 %all-reduce.1 = f32[4]{0:T(128)S(1)} all-reduce(f32[4]{0:T(128)S(1)} %dynamic-update-slice.1), channel_id=1, replica_groups=mesh['dp_0'=4,'dp_1'=4,'dp_2'=4,'dp_3'=2,'mp'=4] {'dp_1'}, use_global_device_ids=true, to_apply=%add.1 | all-reduce | flops 4 | bytes 32
  175.9 1.4 dynamic-update-slice.2
  178.5 13.5 %all-reduce.2 = f32[4]{0:T(128)S(1)} all-reduce(f32[4]{0:T(128)S(1)} %dynamic-update-slice.2), channel_id=1, replica_groups=mesh['dp_0'=4,'dp_1'=4,'dp_2'=4,'dp_3'=2,'mp'=4] {'dp_2'}, use_global_device_ids=true, to_apply=%add.2 | all-reduce | flops 4 | bytes 32
  192.6 1.4 dynamic-update-slice.3
  195.3 2.4 %all-reduce.3 = f32[2]{0:T(128)S(1)} all-reduce(f32[2]{0:T(128)S(1)} %dynamic-update-slice.3), channel_id=1, replica_groups=mesh['dp_0'=4,'dp_1'=4,'dp_2'=4,'dp_3'=2,'mp'=4] {'dp_3'}, use_global_device_ids=true, to_apply=%add.3 | all-reduce | flops 2 | bytes 16
  198.3 1.4 dynamic-update-slice.4
  199.7 11.6 %all-reduce.4 = f32[4]{0:T(128)S(1)} all-reduce(f32[4]{0:T(128)S(1)} %dynamic-update-slice.4), channel_id=1, replica_groups=mesh['dp_0'=4,'dp_1'=4,'dp_2'=4,'dp_3'=2,'mp'=4] {'mp'}, use_global_device_ids=true, to_apply=%add.4 | all-reduce | flops 4 | bytes 32
  212.6 2.0 multiply_multiply_fusion
  (34 shorter events, 14.5 us)
Async XLA Ops:
  7.2 126.4 %all-gather.3.cloned.1.call-start = ((), (), s32[]{:S(2)}) async-start(), calls=%async_computation.4 | async-start | bytes 4227072 | tf_op jit(solution)/shard_map/all_gather | solution.py:56
  10.0 13.3 %all-to-all-start.1 = ((bf16[4,4,2048]{2,1,0:T(4,128)(2,1)}), bf16[4,4,2048]{2,1,0:T(4,128)(2,1)S(1)}, u32[]{:S(2)}, u32[]{:S(2)}) async-start(bf16[4,4,2048]{2,1,0:T(4,128)(2,1)} %broadcast_in_dim.2), calls=%async_computation.1 | async-start | bytes 131072 | tf_op jit(solution)/shard_map/all_to_all | solution.py:24
  27.7 34.7 %all-to-all-start = ((bf16[128,2,128]{2,1,0:T(2,128)(2,1)}), bf16[128,2,128]{2,1,0:T(2,128)(2,1)S(1)}, u32[]{:S(2)}, u32[]{:S(2)}) async-start(bf16[128,2,128]{2,1,0:T(2,128)(2,1)} %reshape.45), calls=%async_computation | async-start | bytes 131072 | tf_op jit(solution)/shard_map/all_to_all | solution.py:93
  62.4 23.5 %all-to-all-start.3 = ((bf16[64,2,256]{2,1,0:T(2,128)(2,1)}), bf16[64,2,256]{2,1,0:T(2,128)(2,1)S(1)}, u32[]{:S(2)}, u32[]{:S(2)}) async-start(bf16[64,2,256]{2,1,0:T(2,128)(2,1)} %reshape.49), calls=%async_computation.3 | async-start | bytes 131072 | tf_op jit(solution)/shard_map/all_to_all | solution.py:40
  140.5 5.2 %copy-start = (bf16[512,4096]{1,0:T(8,128)(2,1)S(1)}, bf16[512,4096]{1,0:T(8,128)(2,1)}, u32[]{:S(2)}) copy-start(bf16[512,4096]{1,0:T(8,128)(2,1)} %reshape.34) | copy-start | bytes 12582916
Sparse Core Ops, SparseCore 0:
  13.0 120.5 all-gather.2
